TPU v7x, 32 devices: a whole 2x2x4 slice. The times are simulated.
32 devices in a mesh: grp: 2 (over x), row: 8 (over z, y), col: 2 (over core).
Axes of the slice: x: 2, y: 2, z: 4, core: 2. Of those that a mesh axis runs over, the one named last changes fastest.
Arguments:
- density: bfloat16 [1024, 32, 128], P(('grp', 'row', 'col')), parts along dimension 0, may hold values from -6 to 6
- leaf_target: int32 [1024], P(('grp', 'row', 'col')), parts along dimension 0, may hold values from 0 to 511, as said below
- geometry: float32 [6, 131072], P(None, ('grp', 'row', 'col')), parts along dimension 1, may hold values from -6 to 6
- near_list: int32 [1024, 16], P(('grp', 'row', 'col')), parts along dimension 0, may hold values from -1 to 511, as said below
- far_list: int32 [1024, 16], P(('grp', 'row', 'col')), parts along dimension 0, may hold values from -1 to 511, as said below
- node_list: int32 [128, 32], P(('grp', 'row', 'col')), parts along dimension 0, may hold values from -1 to 63, as said below
- basis_in: bfloat16 [1024, 64, 128], P(('grp', 'row', 'col')), parts along dimension 0, may hold values from -0.5 to 0.5
- basis_out: bfloat16 [1024, 64, 128], P(('grp', 'row', 'col')), parts along dimension 0, may hold values from -0.75 to 0.75
- transfer: bfloat16 [128, 64, 512], P(('grp', 'row', 'col')), parts along dimension 0, may hold values from -0.25 to 0.25
- node_points: float32 [3, 8192], P(None, 'grp'), parts along dimension 1, may hold values from -6 to 6
Outputs:
- potential: bfloat16 [1024, 32, 128], P(('grp', 'row', 'col')), parts along dimension 0
There are 2 independent parts, one for each index of `grp`. A program takes and returns all parts, laid end to end along the dimension named above; each array names one. Nothing has to cross between parts.
Inputs may be any that keep to these rules, and one draw needn't show every extreme that they name: `leaf_target`: A permutation of the tree positions; of the 32 slab leaves of one device, exactly 2 go to the block of 32 tree positions of each device. `near_list`: row t holds t in slot 0; every other slot holds either -1 or a leaf other than t within 16 of t, the leaves of a row distinct; a -1 may stand in any slot after slot 0, also between leaves. `far_list`: every slot of row t holds either -1 or a leaf within 16 of t that is neither t nor in row t of near_list, the leaves of a row distinct; a -1 may stand in any slot, also between leaves. `node_list`: row p holds distinct nodes that differ from p by more than 2, then -1 in the unused slots.
All inputs are finite; a program needn't handle non-finite values.
Results may differ from a plain program's by a relative error of at most 0.0053.
Values may be sent and summed in bfloat16 or wider, within the bound.
A program may use at most 64 MiB of HBM per device.

v0:
```python
import functools
import math

import jax
import jax.numpy as jnp
from jax import lax
from jax.experimental import pallas as pl
from jax.experimental.pallas import tpu as pltpu
from jax.sharding import PartitionSpec as P

REACH = 16
smoothing = 0.1
inv_four_pi = 0.25 / math.pi
NT = (((1,), (1,)), ((), ()))


def compacted(entries, base, pad):
    live = entries >= 0
    place = jnp.cumsum(live.astype(jnp.int32), axis=1) - 1
    slots = jnp.arange(entries.shape[1], dtype=jnp.int32)
    hit = live[:, :, None] & (place[:, :, None] == slots)
    return (
        jnp.max(jnp.where(hit, (entries + base)[:, :, None], -1), axis=1),
        pad,
        jnp.sum(live.astype(jnp.int32), axis=1),
    )


def fill(packed):
    rows, pad, count = packed
    return jnp.where(rows < 0, pad, rows), count


def thirds(a):
    high = a.astype(jnp.bfloat16).astype(jnp.float32)
    rest = a - high
    mid = rest.astype(jnp.bfloat16).astype(jnp.float32)
    return high, mid, rest - mid


def left_side(a):
    h, m, l = thirds(a)
    return jnp.concatenate([h, m, h, l, h, m], axis=0)


def right_side(a):
    h, m, l = thirds(a)
    return jnp.concatenate([h, h, m, h, l, m], axis=0)


def point_forms(points, row):
    xyz = jnp.where(row < 3, points, 0.0)
    square = jnp.sum(xyz * xyz, axis=0, keepdims=True)
    target = jnp.where(row < 3, points, jnp.where(row == 3, square, jnp.where(row == 4, 1.0, 0.0)))
    source = jnp.where(
        row < 3,
        -2.0 * points,
        jnp.where(row == 3, 1.0, jnp.where(row == 4, square + smoothing * smoothing, 0.0)),
    )
    return xyz, target, source


def flat(count, chunk, size):
    rows = count.shape[0]
    chunks = (count + chunk - 1) // chunk
    row_ids = jnp.arange(rows, dtype=jnp.int32)
    end = jnp.sum(jnp.where(row_ids[:, None] >= row_ids, chunks, 0), axis=1)
    g = jnp.arange(size, dtype=jnp.int32)
    row = jnp.sum((end <= g[:, None]).astype(jnp.int32), axis=1)
    start = jnp.sum(jnp.where(row_ids == row[:, None], end - chunks, 0), axis=1)
    return row, jnp.where(row < rows, (g - start) * chunk, 0), jnp.sum(chunks).reshape(1)


def field_kernel(
    wide, nodes, chunk,
    near_idx, near_row, near_col, near_total, far_idx, far_row, far_col, far_total, first_node,
    geo, dens, skel, node_pts, node_skel, transfer, basis_out, out,
    target_form, source_form, far_target, far_form, far_skel, near_acc, far_acc, both, near_k, square, far_k,
):
    leaves, nrhs, leaf_size = out.shape
    nodes_here, rank, width = transfer.shape
    children = width // rank
    bf16, f32 = jnp.bfloat16, jnp.float32
    row = lax.broadcasted_iota(jnp.int32, (8, leaf_size), 0)
    lane = lax.broadcasted_iota(jnp.int32, (1, leaf_size), 1)
    low = lane < rank
    base = wide + 1
    group = 4

    def columns(ref, block):
        return ref[:, pl.ds(pl.multiple_of(block * leaf_size, leaf_size), leaf_size)]

    def each(count, body):
        def step(i, carry):
            for k in range(group):
                body(i * group + k)
            return carry

        lax.fori_loop(0, count // group, step, 0)

    def node_block(b):
        _, _, source = point_forms(columns(node_pts, b), row)
        form = right_side(source)
        turned = pltpu.roll(form, rank, 1)
        far_form[0, base + 2 * b] = jnp.where(low, form, 0.0).astype(bf16)
        far_form[1, base + 2 * b] = jnp.where(low, 0.0, turned).astype(bf16)
        far_form[0, base + 2 * b + 1] = jnp.where(low, turned, 0.0).astype(bf16)
        far_form[1, base + 2 * b + 1] = jnp.where(low, 0.0, form).astype(bf16)

    each(nodes // 2, node_block)

    def spread(skel_ref, first):
        def step(s):
            both_halves = jnp.concatenate([skel_ref[s], skel_ref[s]], axis=1)
            none = jnp.zeros_like(both_halves)
            far_skel[0, first + s] = jnp.where(low, both_halves, none)
            far_skel[1, first + s] = jnp.where(low, none, both_halves)

        each(skel_ref.shape[0], step)

    spread(node_skel, base)
    spread(skel, 0)
    far_skel[0, wide] = jnp.zeros((nrhs, leaf_size), bf16)
    far_skel[1, wide] = jnp.zeros((nrhs, leaf_size), bf16)

    for b in range(nodes_here // 2):
        _, target, _ = point_forms(columns(node_pts, first_node[0] // 2 + b), row)
        turned = left_side(target).T.astype(bf16)
        far_target[leaves + 2 * b] = turned[:rank]
        far_target[leaves + 2 * b + 1] = turned[rank:]

    def leaf_block(s):
        points = columns(geo, s)
        xyz, target, source = point_forms(points, row)
        normal = jnp.where(row < 3, pltpu.roll(points, 5, 0), 0.0) * inv_four_pi
        shift = -jnp.sum(normal * xyz, axis=0, keepdims=True)
        normal = jnp.where(row == 4, shift, normal)
        form = right_side(source)
        source_form[s] = jnp.concatenate([form, right_side(normal)], axis=1).astype(bf16)
        far_form[0, s] = jnp.where(low, form, 0.0).astype(bf16)
        far_form[1, s] = jnp.where(low, 0.0, pltpu.roll(form, rank, 1)).astype(bf16)

    each(wide, leaf_block)
    source_form[wide] = source_form[0]
    far_form[0, wide] = far_form[0, 0]
    far_form[1, wide] = far_form[1, 0]

    def own_block(t):
        _, target, _ = point_forms(columns(geo, t + REACH), row)
        turned = left_side(target).T.astype(bf16)
        target_form[t] = turned
        far_target[t] = turned[:rank]
        near_acc[t] = jnp.zeros((nrhs, leaf_size), f32)
        far_acc[t] = jnp.zeros((nrhs, rank), f32)

    each(leaves, own_block)
    for p in range(nodes_here):
        far_acc[leaves + p] = jnp.zeros((nrhs, rank), f32)

    def pipeline(idx, rows_of, cols_of, total, rows, first, middle, last):
        def ids_of(g):
            t, c = jnp.minimum(rows_of[g], rows - 1), cols_of[g]
            return t, [idx[t, c + k] for k in range(chunk)]

        def step(g, carry):
            old = jnp.maximum(g - 2, 0)
            last(jnp.where(g >= 2, rows_of[old], rows), ids_of(old)[1])
            middle()
            first(*ids_of(g))
            return carry

        lax.fori_loop(0, total[0] + 2, step, 0)

    def far_first(t, ids):
        weights = jnp.concatenate(
            [far_form[0, ids[k]] + far_form[1, ids[k + 1]] for k in range(0, chunk, 2)], axis=1
        )
        square[...] = jnp.dot(far_target[t], weights, preferred_element_type=f32)

    def far_middle():
        far_k[...] = (inv_four_pi * lax.rsqrt(square[...])).astype(bf16)

    def far_last(t, ids):
        charge = jnp.concatenate(
            [far_skel[0, ids[k]] + far_skel[1, ids[k + 1]] for k in range(0, chunk, 2)], axis=1
        )
        far_acc[t] += lax.dot_general(charge, far_k[...], NT, preferred_element_type=f32)

    pipeline(
        far_idx, far_row, far_col, far_total, leaves + nodes_here, far_first, far_middle, far_last
    )

    def near_first(t, ids):
        form = target_form[t]
        for k in range(chunk):
            both[k] = jnp.dot(form, source_form[ids[k]], preferred_element_type=f32)

    def near_middle():
        for k in range(chunk):
            r = lax.rsqrt(both[k, :, :leaf_size])
            near_k[:, k * leaf_size : (k + 1) * leaf_size] = (
                both[k, :, leaf_size:] * (r * r * r)
            ).astype(bf16)

    def near_last(t, ids):
        charge = jnp.concatenate([dens[ids[k]] for k in range(chunk)], axis=1)
        near_acc[t] += lax.dot_general(charge, near_k[...], NT, preferred_element_type=f32)

    pipeline(
        near_idx, near_row, near_col, near_total, leaves, near_first, near_middle, near_last
    )

    for p in range(nodes_here):
        far = far_acc[leaves + p].astype(bf16)
        spreading = jnp.dot(far, transfer[p], preferred_element_type=f32)
        for c in range(children):
            t = p * children + c
            local = (far_acc[t] + spreading[:, c * rank : (c + 1) * rank]).astype(bf16)
            out[t] = (
                near_acc[t] + jnp.dot(local, basis_out[t], preferred_element_type=f32)
            ).astype(bf16)


def field(near, far, node, first_node, geo, dens, skel, node_pts, node_skel, transfer, basis_out):
    wide, nodes = skel.shape[0], node_skel.shape[0]
    nrhs, leaf_size = dens.shape[1:]
    nodes_here, rank, width = transfer.shape
    leaves = basis_out.shape[0]
    terms, chunk = 48, 4
    bf16, f32 = jnp.bfloat16, jnp.float32
    near_idx, near_count = near
    far_idx, far_count = far
    node_idx, node_count = node
    slots = node_idx.shape[1]
    far_size = (far_idx.size + node_idx.size) // chunk + 2
    far_idx = jnp.concatenate(
        [
            jnp.pad(far_idx, ((0, 0), (0, slots - far_idx.shape[1])), constant_values=wide),
            node_idx,
        ],
        axis=0,
    )
    far_count = jnp.concatenate([far_count, node_count])
    smem = pl.BlockSpec(memory_space=pltpu.SMEM)
    vmem = pl.BlockSpec(memory_space=pltpu.VMEM)
    return pl.pallas_call(
        functools.partial(field_kernel, wide, nodes, chunk),
        out_shape=jax.ShapeDtypeStruct((leaves, nrhs, leaf_size), bf16),
        in_specs=[smem] * 9 + [vmem] * 7,
        out_specs=vmem,
        scratch_shapes=[
            pltpu.VMEM((leaves, leaf_size, terms), bf16),
            pltpu.VMEM((wide + 1, terms, 2 * leaf_size), bf16),
            pltpu.VMEM((leaves + nodes_here, rank, terms), bf16),
            pltpu.VMEM((2, wide + 1 + nodes, terms, leaf_size), bf16),
            pltpu.VMEM((2, wide + 1 + nodes, nrhs, leaf_size), bf16),
            pltpu.VMEM((leaves + 1, nrhs, leaf_size), f32),
            pltpu.VMEM((leaves + nodes_here + 1, nrhs, rank), f32),
            pltpu.VMEM((chunk, leaf_size, 2 * leaf_size), f32),
            pltpu.VMEM((leaf_size, chunk * leaf_size), bf16),
            pltpu.VMEM((rank, chunk * rank), f32),
            pltpu.VMEM((rank, chunk * rank), bf16),
        ],
        compiler_params=pltpu.CompilerParams(vmem_limit_bytes=48 * 1024 * 1024),
        name="field",
    )(
        near_idx, *flat(near_count, chunk, near_idx.size // chunk + 2),
        far_idx, *flat(far_count, chunk, far_size),
        first_node, geo, dens, skel, node_pts, node_skel, transfer, basis_out,
    )


def peers():
    columns = lax.axis_size("col")
    count = lax.axis_size("row") * columns
    me = lax.axis_index("row") * columns + lax.axis_index("col")

    def peer(k):
        q = lax.rem(me + k, count)
        return q, {"row": q // columns, "col": lax.rem(q, columns)}

    return me, count, peer


def greet(count, peer):
    barrier = pltpu.get_barrier_semaphore()
    for k in range(1, count):
        pl.semaphore_signal(
            barrier, inc=1, device_id=peer(k)[1], device_id_type=pl.DeviceIdType.MESH
        )
    pl.semaphore_wait(barrier, count - 1)


def sender(send_sem, recv_sem):
    copies = []

    def send(src, dst, where):
        k = len(copies)
        copy = pltpu.make_async_remote_copy(
            src_ref=src,
            dst_ref=dst,
            send_sem=send_sem.at[k],
            recv_sem=recv_sem.at[k],
            device_id=where,
            device_id_type=pl.DeviceIdType.MESH,
        )
        copy.start()
        copies.append(copy)

    return copies, send


def exchange_kernel(outgoing, slots, geo, arrived, arrived_slots, geo_wide, send_sem, recv_sem):
    me, count, peer = peers()
    per = outgoing.shape[0] // count
    inner = geo.shape[1]
    halo = (geo_wide.shape[1] - inner) // 2
    greet(count, peer)
    copies, send = sender(send_sem, recv_sem)
    for k in range(1, count):
        q, where = peer(k)
        send(slots.at[q], arrived_slots.at[me], where)
        send(outgoing.at[pl.ds(q * per, per)], arrived.at[pl.ds(me * per, per)], where)
    send(geo.at[:, pl.ds(inner - halo, halo)], geo_wide.at[:, pl.ds(0, halo)], peer(1)[1])
    send(geo.at[:, pl.ds(0, halo)], geo_wide.at[:, pl.ds(halo + inner, halo)], peer(count - 1)[1])
    arrived_slots[me] = slots[me]
    for k in range(per):
        arrived[me * per + k] = outgoing[me * per + k]
    geo_wide[:, halo : halo + inner] = geo[...]
    for copy in copies:
        copy.wait()


def share_kernel(dens, skel, node_skel, dens_wide, skel_wide, all_skel, send_sem, recv_sem):
    me, count, peer = peers()
    leaves, here = dens.shape[0], node_skel.shape[0]
    greet(count, peer)
    copies, send = sender(send_sem, recv_sem)
    for own, wide in ((dens, dens_wide), (skel, skel_wide)):
        send(own.at[pl.ds(leaves - REACH, REACH)], wide.at[pl.ds(0, REACH)], peer(1)[1])
        send(own.at[pl.ds(0, REACH)], wide.at[pl.ds(REACH + leaves, REACH)], peer(count - 1)[1])
    for k in range(1, count):
        send(node_skel, all_skel.at[pl.ds(me * here, here)], peer(k)[1])
    dens_wide[REACH : REACH + leaves] = dens[...]
    dens_wide[leaves + 2 * REACH] = jnp.zeros(dens.shape[1:], dens.dtype)
    skel_wide[REACH : REACH + leaves] = skel[...]
    for k in range(here):
        all_skel[me * here + k] = node_skel[k]
    for copy in copies:
        copy.wait()


def remote(kernel, name, number, copies, outs, *operands):
    vmem = pl.BlockSpec(memory_space=pltpu.VMEM)
    return pl.pallas_call(
        kernel,
        out_shape=[jax.ShapeDtypeStruct(*o) for o in outs],
        in_specs=[vmem] * len(operands),
        out_specs=[vmem] * len(outs),
        scratch_shapes=[pltpu.SemaphoreType.DMA((copies,)), pltpu.SemaphoreType.DMA((copies,))],
        compiler_params=pltpu.CompilerParams(collective_id=number, has_side_effects=True),
        name=name,
    )(*operands)


def on_device(
    density,
    leaf_target,
    geometry,
    near_list,
    far_list,
    node_list,
    basis_in,
    basis_out,
    transfer,
    node_points,
):
    leaves, nrhs_here, leaf_size = density.shape
    rank_size = basis_in.shape[1]
    nodes_here = transfer.shape[0]
    children = leaves // nodes_here
    wide = leaves + 2 * REACH
    first_leaf = lax.axis_index(("row", "col")) * leaves
    destination = leaf_target // leaves
    tree_slot = leaf_target % leaves
    count = lax.axis_size("row") * lax.axis_size("col")
    per = leaves // count
    ids = jnp.arange(leaves, dtype=jnp.int32)
    earlier = (destination[:, None] == destination) & (ids[:, None] > ids)
    rank = destination * per + jnp.sum(earlier.astype(jnp.int32), axis=1)
    placed = rank == ids[:, None]
    outgoing = density[jnp.sum(jnp.where(placed, ids, 0), axis=1)]
    out_slot = jnp.sum(jnp.where(placed, tree_slot, 0), axis=1).reshape(count, 1, per)
    bf16, f32 = jnp.bfloat16, jnp.float32
    arrived, arrived_slot, geo_wide = remote(
        exchange_kernel,
        "exchange",
        0,
        2 * count,
        (
            (density.shape, bf16),
            ((count, 1, leaf_size), jnp.int32),
            ((8, wide * leaf_size), f32),
        ),
        outgoing,
        jnp.pad(out_slot, ((0, 0), (0, 0), (0, leaf_size - per))),
        jnp.pad(geometry, ((0, 2), (0, 0))),
    )
    landed = arrived_slot[:, 0, :per].reshape(leaves)
    ordered = arrived[jnp.sum(jnp.where(landed == ids[:, None], ids, 0), axis=1)]
    skeleton = jnp.einsum(
        "tnl,trl->tnr", ordered, basis_in, preferred_element_type=jnp.float32
    ).astype(jnp.bfloat16)
    stacked = (
        skeleton.reshape(nodes_here, children, nrhs_here, rank_size)
        .transpose(0, 2, 1, 3)
        .reshape(nodes_here, nrhs_here, children * rank_size)
    )
    node_skel = jnp.einsum(
        "pnk,prk->pnr", stacked, transfer, preferred_element_type=jnp.float32
    ).astype(jnp.bfloat16)
    dens_wide, skel_wide, all_skel = remote(
        share_kernel,
        "share",
        1,
        count + 3,
        (
            ((wide + 1, nrhs_here, leaf_size), bf16),
            ((wide, nrhs_here, rank_size), bf16),
            ((nodes_here * count, nrhs_here, rank_size), bf16),
        ),
        ordered,
        skeleton,
        node_skel,
    )
    near = fill(compacted(near_list, REACH - first_leaf, wide))
    far = fill(compacted(far_list, REACH - first_leaf, wide))
    node = fill(compacted(node_list, wide + 1, wide))
    first_node = (first_leaf // children).reshape(1)
    node_pts = jnp.pad(node_points, ((0, 5), (0, 0)))
    return field(
        near, far, node, first_node, geo_wide, dens_wide, skel_wide, node_pts, all_skel,
        transfer, basis_out,
    )


def solution(mesh):
    return jax.shard_map(
        on_device,
        mesh=mesh,
        in_specs=(
            P(("grp", "row", "col"), None, None),
            P(("grp", "row", "col")),
            P(None, ("grp", "row", "col")),
            P(("grp", "row", "col"), None),
            P(("grp", "row", "col"), None),
            P(("grp", "row", "col"), None),
            P(("grp", "row", "col"), None, None),
            P(("grp", "row", "col"), None, None),
            P(("grp", "row", "col"), None, None),
            P(None, "grp"),
        ),
        out_specs=P(("grp", "row", "col"), None, None),
        check_vma=False,
    )
```

profile of v0, /device:TPU:3, one launch (start us, length us, event | category | flops | bytes accessed | tf_op | source)
XLA Modules:
  0.0 107.3 jit_solution(8881820502420078532)
XLA Ops:
  0.0 0.7 copy-done.14
  0.7 0.2 convert_reduce_fusion.2
  1.1 2.3 %gather_fusion = bf16[32,32,128]{2,1,0:T(8,128)(2,1)} fusion(bf16[32,32,128]{2,1,0:T(8,128)(2,1)} %param.10, s32[1024]{0:T(1024)S(1)} %pad_clamp_fusion.1), kind=kCustom, calls=%fused_computation | custom fusion | bytes 524416 | tf_op jit(solution)/shard_map/gather | solution.py:392
  3.4 0.6 pad.17.slots
  4.0 0.7 pad.18.geo
  4.7 12.2 %exchange.1 = (bf16[32,32,128]{2,1,0:T(8,128)(2,1)}, s32[16,1,128]{2,1,0:T(1,128)}, f32[8,8192]{1,0:T(8,128)}) custom-call(bf16[32,32,128]{2,1,0:T(8,128)(2,1)} %gather_fusion, s32[16,1,128]{2,1,0:T(1,128)} %pad.17.slots, f32[8,4096]{1,0:T(8,128)} %pad.18.geo), custom_call_target="tpu_custom_call" | custom-call | tf_op jit(solution)/shard_map/exchange/pallas_call | solution.py:355
  16.9 0.7 slice_reduce_fusion
  17.8 1.6 %gather_fusion.1 = bf16[32,32,128]{2,1,0:T(8,128)(2,1)S(1)} fusion(bf16[32,32,128]{2,1,0:T(8,128)(2,1)} %get-tuple-element.12, s32[1024]{0:T(1024)S(1)} %pad_clamp_fusion), kind=kCustom, calls=%fused_computation.1 | custom fusion | bytes 524416 | tf_op jit(solution)/shard_map/gather | solution.py:410
  19.4 0.4 convolution_convert_fusion.skel
  19.8 0.3 copy-done.7
  20.2 0.6 copy-done.8
  20.8 0.2 reshape.84
  21.0 0.7 copy-done.1
  21.8 0.8 convolution_convert_fusion.1.node_skel
  22.6 22.1 %share.1 = (bf16[65,32,128]{2,1,0:T(8,128)(2,1)}, bf16[64,32,64]{2,1,0:T(8,128)(2,1)}, bf16[64,32,64]{2,1,0:T(8,128)(2,1)}) custom-call(bf16[32,32,128]{2,1,0:T(8,128)(2,1)} %copy-done.7, bf16[32,32,64]{2,1,0:T(8,128)(2,1)} %copy-done.8, bf16[4,32,64]{2,1,0:T(8,128)(2,1)} %convolution_convert_fusion.1.node_skel), custom_call_target="tpu_custom_call" | custom-call | tf_op jit(solution)/shard_map/share/pallas_call | solution.py:355
  45.0 0.8 fusion.6
  46.1 0.2 reduce_window_sum.29
  46.6 0.2 reduce_window_sum.30
  46.8 0.1 select_reduce_fusion.2
  47.2 0.7 fusion.7
  48.2 0.2 reduce_window_sum.28
  48.8 1.0 copy-done.4
  49.8 1.0 copy-done.5
  50.8 56.5 %field.1 = bf16[32,32,128]{2,1,0:T(8,128)(2,1)} custom-call(s32[32,16]{1,0:T(8,128)S(1)} %compare_select_fusion.1.near_idx, s32[130]{0:T(256)S(1)} %convert_reduce_fusion.1.near_row, s32[130]{0:T(256)S(1)} %compare_select_fusion.6.near_col, s32[1]{0:T(128)} %bitcast.near_total, s32[36,32]{1,0:T(8,128)S(1)} %select_add_fusion.far_idx, ...), custom_call_target="tpu_custom_call" | custom-call | tf_op jit(solution)/shard_map/field/pallas_call | solution.py:246
  (70 shorter events, 2.3 us)
Async XLA Ops:
  0.0 19.4 %copy-start = (bf16[32,64,128]{2,1,0:T(8,128)(2,1)S(1)}, bf16[32,64,128]{2,1,0:T(8,128)(2,1)}, u32[]{:S(2)}) copy-start(bf16[32,64,128]{2,1,0:T(8,128)(2,1)} %param.16) | copy-start | bytes 1572868
  0.0 0.7 copy-start.14
  1.1 3.0 %copy-start.9 = (f32[6,4096]{1,0:T(8,128)S(1)}, f32[6,4096]{1,0:T(8,128)}, u32[]{:S(2)}) copy-start(f32[6,4096]{1,0:T(8,128)} %param.12) | copy-start | bytes 294916
  19.4 0.7 copy-start.7
  20.1 0.7 copy-start.8
  20.8 0.9 copy-start.1
  21.8 22.9 %copy-start.13 = (s32[4,32]{1,0:T(4,128)S(1)}, s32[4,32]{1,0:T(4,128)}, u32[]{:S(2)}) copy-start(s32[4,32]{1,0:T(4,128)} %param.15) | copy-start | bytes 1540
  21.8 23.0 %copy-start.11 = (s32[32,16]{0,1:T(8,128)S(1)}, s32[32,16]{0,1:T(8,128)}, u32[]{:S(2)}) copy-start(s32[32,16]{0,1:T(8,128)} %param.14) | copy-start | bytes 6148
  22.6 23.5 %copy-start.12 = (s32[32,16]{0,1:T(8,128)S(1)}, s32[32,16]{0,1:T(8,128)}, u32[]{:S(2)}) copy-start(s32[32,16]{0,1:T(8,128)} %param.13) | copy-start | bytes 6148
  22.6 26.1 %copy-start.10 = (f32[3,4096]{1,0:T(4,128)S(1)}, f32[3,4096]{1,0:T(4,128)}, u32[]{:S(2)}) copy-start(f32[3,4096]{1,0:T(4,128)} %param.19) | copy-start | bytes 147460
  22.6 26.2 %copy-start.3 = (bf16[32,64,128]{2,1,0:T(8,128)(2,1)S(1)}, bf16[32,64,128]{2,1,0:T(8,128)(2,1)}, u32[]{:S(2)}) copy-start(bf16[32,64,128]{2,1,0:T(8,128)(2,1)} %basis_out.1) | copy-start | bytes 1572868
  44.6 4.1 %copy-start.2 = (bf16[65,32,128]{2,1,0:T(8,128)(2,1)S(1)}, bf16[65,32,128]{2,1,0:T(8,128)(2,1)}, u32[]{:S(2)}) copy-start(bf16[65,32,128]{2,1,0:T(8,128)(2,1)} %get-tuple-element.14.dens) | copy-start | bytes 1597444
  46.8 1.9 %copy-start.6 = (f32[8,8192]{1,0:T(8,128)S(1)}, f32[8,8192]{1,0:T(8,128)}, u32[]{:S(2)}) copy-start(f32[8,8192]{1,0:T(8,128)} %get-tuple-element.11.geo) | copy-start | bytes 786436
  48.8 1.0 copy-start.4
  49.8 1.0 copy-start.5
where the time goes:
time: 108 us; the launch traced here: 107 us
  Pallas kernels  90.7 us (84%)
  local copies, waits for them, and re-layouts  11.4 us (11%)
  other arithmetic  3.77 us (3%)
  matrix products  1.18 us (1%)
    pallas_call x1, Pallas kernels, field(): pl.pallas_call(functools.partial(field_kernel, wide, nodes, chunk), out_s...  56.5 us
    pallas_call x2, Pallas kernels, remote(): pl.pallas_call(kernel, out_shape=[jax.ShapeDtypeStruct(*o) for o in outs]...  34.2 us
    unnamed x32, local copies, waits for them, and re-layouts  4.64 us
    gather x1, local copies, waits for them, and re-layouts, on_device(): outgoing = density[jnp.sum(jnp.where(placed, ids, 0), axis=1)]  2.27 us

commit v1 on v0

v1 whole, which is shorter than its diff:
```python
import functools
import math

import jax
import jax.numpy as jnp
from jax import lax
from jax.experimental import pallas as pl
from jax.experimental.pallas import tpu as pltpu
from jax.sharding import PartitionSpec as P

REACH = 16
smoothing = 0.1
inv_four_pi = 0.25 / math.pi
NT = (((1,), (1,)), ((), ()))
bf16, f32 = jnp.bfloat16, jnp.float32
EARLY, MIDDLE = 8, 16


def thirds(a):
    high = a.astype(bf16).astype(f32)
    rest = a - high
    mid = rest.astype(bf16).astype(f32)
    return high, mid, rest - mid


def left_side(a):
    h, m, l = thirds(a)
    return jnp.concatenate([h, m, h, l, h, m], axis=0)


def right_side(a):
    h, m, l = thirds(a)
    return jnp.concatenate([h, h, m, h, l, m], axis=0)


def xyz_square(points, row):
    xyz = jnp.where(row < 3, points, 0.0)
    return xyz, jnp.sum(xyz * xyz, axis=0, keepdims=True)


def target_form(points, row):
    _, square = xyz_square(points, row)
    return jnp.where(row < 3, points, jnp.where(row == 3, square, jnp.where(row == 4, 1.0, 0.0)))


def source_form(points, row):
    xyz, square = xyz_square(points, row)
    return xyz, jnp.where(
        row < 3,
        -2.0 * points,
        jnp.where(row == 3, 1.0, jnp.where(row == 4, square + smoothing * smoothing, 0.0)),
    )


def each(lo, hi, group, body):
    while (hi - lo) % group:
        group //= 2

    def step(i, carry):
        for k in range(group):
            body(lo + i * group + k)
        return carry

    lax.fori_loop(0, (hi - lo) // group, step, 0)


def whole_kernel(
    picks, slots, near_list, far_list, node_list, density, geo, node_pts, basis_in_far, transfer_far,
    basis_out_far, out,
    basis_in, transfer, basis_out, local_sem, outgoing, slot_rows, arrived, arrived_rows, geo_wide, dens_wide,
    skel_wide, all_skel, near_src, near_tgt, far_src, far_tgt, far_skel, near_k, far_k, down, send_sem, recv_sem,
):
    leaves, nrhs, size = out.shape
    here, rank, width = transfer.shape
    children = width // rank
    wide = leaves + 2 * REACH
    rows_n, cols_n = lax.axis_size("row"), lax.axis_size("col")
    count = rows_n * cols_n
    per = leaves // count
    nodes = count * here
    base = wide + 1
    my_row, my_col = lax.axis_index("row"), lax.axis_index("col")
    me = my_row * cols_n + my_col
    first_leaf = me * leaves
    inner = geo.shape[1]
    halo = REACH * size
    row = lax.broadcasted_iota(jnp.int32, (8, size), 0)
    lane = lax.broadcasted_iota(jnp.int32, (1, size), 1)
    low = lane < rank

    def peer(k):
        q = lax.rem(me + k, count)
        return q, {"row": q // cols_n, "col": lax.rem(q, cols_n)}

    copies = []

    def send(src, dst, where):
        k = len(copies)
        copy = pltpu.make_async_remote_copy(
            src_ref=src, dst_ref=dst, send_sem=send_sem.at[k], recv_sem=recv_sem.at[k],
            device_id=where, device_id_type=pl.DeviceIdType.MESH,
        )
        copy.start()
        copies.append(copy)
        return copy

    def columns(ref, block):
        return ref[:, pl.ds(pl.multiple_of(block * size, size), size)]

    barrier = pltpu.get_barrier_semaphore()
    for k in range(1, count):
        pl.semaphore_signal(barrier, inc=1, device_id=peer(k)[1], device_id_type=pl.DeviceIdType.MESH)
    fetches = []
    for k, (src, dst) in enumerate(
        ((basis_in_far, basis_in), (transfer_far, transfer), (basis_out_far, basis_out))
    ):
        fetch = pltpu.make_async_copy(src, dst, local_sem.at[k])
        fetch.start()
        fetches.append(fetch)

    for j in range(leaves):
        outgoing[j] = density[jnp.clip(picks[j], 0, leaves - 1)]
    for q in range(count):
        line = jnp.zeros((1, size), jnp.int32)
        for k in range(per):
            line = line + jnp.where(lane == slots[q * per + k], me * per + k + 1, 0)
        slot_rows[q] = line
    geo_wide[0:6, halo : halo + inner] = geo[...]

    def turned(form):
        rest = jnp.zeros((size - form.shape[0], size), f32)
        return jnp.concatenate([form, rest], axis=0).T

    def store_far_source(index, low_form):
        far_src[0, index] = low_form.astype(bf16)
        far_src[1, index] = pltpu.roll(low_form, rank, 1).astype(bf16)

    def node_block(b):
        _, source = source_form(
            jnp.concatenate([columns(node_pts, b), jnp.zeros((5, size), f32)], axis=0), row
        )
        form = turned(right_side(source))
        store_far_source(base + 2 * b, form[:rank])
        store_far_source(base + 2 * b + 1, form[rank:])

    each(0, nodes // 2, 4, node_block)

    pl.semaphore_wait(barrier, count - 1)
    geo_copies = [
        send(geo.at[:, pl.ds(inner - halo, halo)], geo_wide.at[pl.ds(0, 6), pl.ds(0, halo)], peer(1)[1]),
        send(geo.at[:, pl.ds(0, halo)], geo_wide.at[pl.ds(0, 6), pl.ds(halo + inner, halo)], peer(count - 1)[1]),
    ]
    exchange = []
    for k in range(1, count):
        q, where = peer(k)
        exchange.append(send(slot_rows.at[q], arrived_rows.at[me], where))
        exchange.append(
            send(outgoing.at[pl.ds(q * per, per)], arrived.at[pl.ds(me * per, per)], where)
        )
    arrived_rows[me] = slot_rows[me]
    for k in range(per):
        arrived[me * per + k] = outgoing[me * per + k]

    def store_far_target(index, low_form, high_form):
        gap = jnp.zeros((rank - low_form.shape[0], size), f32)
        none = jnp.zeros((2 * rank, size), f32)
        block = jnp.concatenate([low_form, gap, high_form, gap], axis=0)
        far_tgt[index] = jnp.concatenate(
            [jnp.concatenate([block, none], axis=0), jnp.concatenate([none, block], axis=0)], axis=1
        ).astype(bf16)

    def target_block(t):
        form = left_side(target_form(columns(geo_wide, t + REACH), row))
        terms = form.shape[0]
        near_tgt[t] = jnp.concatenate(
            [
                jnp.concatenate([form, jnp.zeros((size - terms, size), f32)], axis=0),
                jnp.concatenate(
                    [jnp.zeros((terms, size), f32), form, jnp.zeros((size - 2 * terms, size), f32)], axis=0
                ),
            ],
            axis=1,
        ).astype(bf16)
        store_far_target(t, jnp.where(low, form, 0.0), jnp.where(low, 0.0, pltpu.roll(form, rank, 1)))

    def source_block(s):
        points = columns(geo_wide, s)
        xyz, source = source_form(points, row)
        normal = jnp.where(row < 3, pltpu.roll(points, 5, 0), 0.0) * inv_four_pi
        shift = -jnp.sum(normal * xyz, axis=0, keepdims=True)
        normal = jnp.where(row == 4, shift, normal)
        left = right_side(source)
        form = turned(jnp.concatenate([left, right_side(normal)], axis=0))
        near_src[s] = form.astype(bf16)
        store_far_source(s, jnp.where(lane < left.shape[0], form[:rank], 0.0))

    each(0, leaves, 4, target_block)
    for b in range(here // 2):
        form = left_side(
            target_form(
                jnp.concatenate(
                    [columns(node_pts, me * (here // 2) + b), jnp.zeros((5, size), f32)], axis=0
                ),
                row,
            )
        )
        other = pltpu.roll(form, rank, 1)
        store_far_target(leaves + 2 * b, jnp.where(low, form, 0.0), jnp.where(low, 0.0, other))
        store_far_target(leaves + 2 * b + 1, jnp.where(low, other, 0.0), jnp.where(low, 0.0, form))
    each(REACH, REACH + leaves, 4, source_block)
    for copy in geo_copies:
        copy.wait_recv()
    each(0, REACH, 4, source_block)
    each(REACH + leaves, wide, 4, source_block)

    def within(entry, shift, pad, least, end):
        return jnp.where(entry < 0, pad, jnp.clip(entry + shift, least, end - 1))

    def near_place(t, k, pad):
        return within(near_list[t, k], REACH - first_leaf, pad, 0, wide)

    def far_place(t, k, pad):
        return within(far_list[t, k], REACH - first_leaf, pad, 0, wide)

    def node_place(p, k, pad):
        return within(node_list[p, k], base, pad, base - 1, base + nodes)

    def couple(weights, ids, store):
        for g in range(len(ids) // 4):
            i = ids[4 * g : 4 * g + 4]
            points = jnp.concatenate(
                [far_src[0, i[0]] + far_src[1, i[1]], far_src[0, i[2]] + far_src[1, i[3]]], axis=1
            )
            square = jnp.dot(points, weights, preferred_element_type=f32)
            store(g, (inv_four_pi * lax.rsqrt(square)).astype(bf16))

    far_slots, node_slots = far_list.shape[1], node_list.shape[1]
    per_tile = 16
    tiles = node_slots // per_tile

    def couple_leaf(t):
        def store(g, value):
            far_k[t, g * rank : (g + 1) * rank] = value

        couple(far_tgt[t], [far_place(t, k, t + REACH) for k in range(far_slots)], store)

    def couple_node(p):
        def store(g, value):
            tile, part = g // 4, g % 4
            far_k[leaves + p * tiles + tile, part * rank : (part + 1) * rank] = value

        own = base + me * here + p
        couple(far_tgt[leaves + p], [node_place(p, k, own) for k in range(node_slots)], store)

    each(0, here, 2, couple_node)
    each(0, leaves, 4, couple_leaf)

    near_slots = near_list.shape[1]

    def near_leaf(t):
        weights = near_tgt[t]
        for k in range(near_slots):
            both = jnp.dot(near_src[near_place(t, k, t + REACH)], weights, preferred_element_type=f32)
            r = lax.rsqrt(both[:, :size])
            near_k[t, k * size : (k + 1) * size] = (both[:, size:] * (r * r * r)).astype(bf16)

    each(0, EARLY, 4, near_leaf)

    for copy in exchange:
        copy.wait_recv()
    place = arrived_rows[0]
    for q in range(1, count):
        place = place + arrived_rows[q]
    for s in range(leaves):
        source = jnp.max(jnp.where(lane == s, place, 0)) - 1
        dens_wide[REACH + s] = arrived[jnp.clip(source, 0, leaves - 1)]
    dens_wide[wide] = jnp.zeros((nrhs, size), bf16)
    for fetch in fetches[:2]:
        fetch.wait()

    def skeleton(i):
        pair = [
            lax.dot_general(
                dens_wide[REACH + 2 * i + c], basis_in[2 * i + c], NT, preferred_element_type=f32
            )
            for c in range(2)
        ]
        skel_wide[REACH // 2 + i] = jnp.concatenate(pair, axis=1).astype(bf16)

    each(0, leaves // 2, 4, skeleton)
    second = [
        send(dens_wide.at[pl.ds(leaves, REACH)], dens_wide.at[pl.ds(0, REACH)], peer(1)[1]),
        send(dens_wide.at[pl.ds(REACH, REACH)], dens_wide.at[pl.ds(REACH + leaves, REACH)], peer(count - 1)[1]),
    ]
    pairs_here = here // 2
    for b in range(pairs_here):
        pair = []
        for c in range(2):
            p = 2 * b + c
            first = REACH // 2 + p * children // 2
            stacked = jnp.concatenate([skel_wide[first + j] for j in range(children // 2)], axis=1)
            pair.append(lax.dot_general(stacked, transfer[p], NT, preferred_element_type=f32))
        all_skel[me * pairs_here + b] = jnp.concatenate(pair, axis=1).astype(bf16)
    half = REACH // 2
    second += [
        send(skel_wide.at[pl.ds(leaves // 2, half)], skel_wide.at[pl.ds(0, half)], peer(1)[1]),
        send(skel_wide.at[pl.ds(half, half)], skel_wide.at[pl.ds(half + leaves // 2, half)], peer(count - 1)[1]),
    ]

    def block_of(r, c):
        return all_skel.at[pl.ds((r * cols_n + c) * pairs_here, pairs_here)]

    mine = block_of(my_row, my_col)
    partners = [{"col": lax.rem(my_col + c, cols_n)} for c in range(1, cols_n)]
    along = [
        send(mine, mine, {"row": lax.rem(my_row + k, rows_n)}) for k in range(1, rows_n)
    ]
    second += [send(mine, mine, where) for where in partners]

    each(EARLY, MIDDLE, 4, near_leaf)
    for k in range(1, rows_n):
        along[k - 1].wait_recv()
        block = block_of(lax.rem(my_row + rows_n - k, rows_n), my_col)
        second += [send(block, block, where) for where in partners]
    each(MIDDLE, leaves, 4, near_leaf)
    for copy in second:
        copy.wait_recv()

    def spread(tile, index):
        other = jnp.concatenate([tile[:, rank:], tile[:, :rank]], axis=1)
        none = jnp.zeros_like(tile)
        far_skel[0, index] = jnp.where(low, tile, none)
        far_skel[1, index] = jnp.where(low, none, other)
        far_skel[0, index + 1] = jnp.where(low, other, none)
        far_skel[1, index + 1] = jnp.where(low, none, tile)

    each(0, nodes // 2, 4, lambda i: spread(all_skel[i], base + 2 * i))
    each(0, wide // 2, 4, lambda i: spread(skel_wide[i], 2 * i))
    for v in range(2):
        far_skel[v, wide] = jnp.zeros((nrhs, size), bf16)
    fetches[2].wait()

    def gathered(ids, matrix):
        lines = []
        for p in range(4):
            i = [ids[4 * g + p] for g in range(4)]
            lines.append(
                jnp.concatenate(
                    [far_skel[0, i[0]] + far_skel[1, i[1]], far_skel[0, i[2]] + far_skel[1, i[3]]], axis=1
                )
            )
        result = jnp.dot(jnp.concatenate(lines, axis=0), matrix, preferred_element_type=f32)
        even = result[:nrhs, :size] + result[2 * nrhs : 3 * nrhs, size:]
        odd = result[nrhs : 2 * nrhs, :size] + result[3 * nrhs :, size:]
        return (even + pltpu.roll(odd, rank, 1))[:, :rank]

    for p in range(here):
        ids = [node_place(p, k, wide) for k in range(node_slots)]
        far = sum(
            gathered(ids[i * per_tile : (i + 1) * per_tile], far_k[leaves + p * tiles + i])
            for i in range(tiles)
        ).astype(bf16)
        spreading = jnp.dot(far, transfer[p], preferred_element_type=f32)
        for c in range(children):
            down[p * children + c] = spreading[:, c * rank : (c + 1) * rank]

    def finish(t):
        far = gathered([far_place(t, k, wide) for k in range(far_slots)], far_k[t])
        charge = jnp.concatenate([dens_wide[near_place(t, k, wide)] for k in range(near_slots)], axis=1)
        near = jnp.dot(charge, near_k[t], preferred_element_type=f32)
        local = (far + down[t]).astype(bf16)
        out[t] = (near + jnp.dot(local, basis_out[t], preferred_element_type=f32)).astype(bf16)

    each(0, leaves, 4, finish)
    for copy in copies:
        copy.wait_send()


def on_device(
    density, leaf_target, geometry, near_list, far_list, node_list, basis_in, basis_out, transfer, node_points,
):
    leaves, nrhs, size = density.shape
    rank = basis_in.shape[1]
    here = transfer.shape[0]
    wide = leaves + 2 * REACH
    rows_n, cols_n = lax.axis_size("row"), lax.axis_size("col")
    count = rows_n * cols_n
    nodes = here * count
    per = leaves // count
    destination = leaf_target // leaves
    ids = jnp.arange(leaves, dtype=jnp.int32)
    earlier = (destination[:, None] == destination) & (ids[:, None] > ids)
    order = destination * per + jnp.sum(earlier.astype(jnp.int32), axis=1)
    placed = order == ids[:, None]
    picks = jnp.sum(jnp.where(placed, ids, 0), axis=1)
    slots = jnp.sum(jnp.where(placed, leaf_target % leaves, 0), axis=1)
    tiles = node_list.shape[1] // 16
    n_copies = 2 * (count - 1) + 2 + 4 + (rows_n - 1) + (cols_n - 1) + (rows_n - 1) * (cols_n - 1)
    smem = pl.BlockSpec(memory_space=pltpu.SMEM)
    vmem = pl.BlockSpec(memory_space=pltpu.VMEM)
    away = pl.BlockSpec(memory_space=pl.ANY)
    return pl.pallas_call(
        whole_kernel,
        out_shape=jax.ShapeDtypeStruct((leaves, nrhs, size), bf16),
        in_specs=[smem] * 5 + [vmem] * 3 + [away] * 3,
        out_specs=vmem,
        scratch_shapes=[
            pltpu.VMEM(basis_in.shape, bf16),
            pltpu.VMEM(transfer.shape, bf16),
            pltpu.VMEM(basis_out.shape, bf16),
            pltpu.SemaphoreType.DMA((3,)),
            pltpu.VMEM((leaves, nrhs, size), bf16),
            pltpu.VMEM((count, 1, size), jnp.int32),
            pltpu.VMEM((leaves, nrhs, size), bf16),
            pltpu.VMEM((count, 1, size), jnp.int32),
            pltpu.VMEM((8, wide * size), f32),
            pltpu.VMEM((wide + 1, nrhs, size), bf16),
            pltpu.VMEM((wide // 2, nrhs, size), bf16),
            pltpu.VMEM((nodes // 2, nrhs, size), bf16),
            pltpu.VMEM((wide, size, size), bf16),
            pltpu.VMEM((leaves, size, 2 * size), bf16),
            pltpu.VMEM((2, wide + 1 + nodes, rank, size), bf16),
            pltpu.VMEM((leaves + here, 4 * rank, 4 * rank), bf16),
            pltpu.VMEM((2, wide + 1 + nodes, nrhs, size), bf16),
            pltpu.VMEM((leaves, near_list.shape[1] * size, size), bf16),
            pltpu.VMEM((leaves + here * tiles, 4 * rank, 4 * rank), bf16),
            pltpu.VMEM((leaves, nrhs, rank), f32),
            pltpu.SemaphoreType.DMA((n_copies,)),
            pltpu.SemaphoreType.DMA((n_copies,)),
        ],
        compiler_params=pltpu.CompilerParams(
            collective_id=0, has_side_effects=True, vmem_limit_bytes=58 * 1024 * 1024
        ),
        name="whole",
    )(
        picks, slots, near_list, far_list, node_list, density, geometry, node_points, basis_in, transfer,
        basis_out,
    )


def solution(mesh):
    leaf = ("grp", "row", "col")
    return jax.shard_map(
        on_device,
        mesh=mesh,
        in_specs=(
            P(leaf, None, None), P(leaf), P(None, leaf), P(leaf, None), P(leaf, None), P(leaf, None),
            P(leaf, None, None), P(leaf, None, None), P(leaf, None, None), P(None, "grp"),
        ),
        out_specs=P(leaf, None, None),
        check_vma=False,
    )
```

time: 108 us -> 54.3 us (0.50)
  the two profiles are of different devices: /device:TPU:3 before, /device:TPU:0 now
where the time goes in v1:
time: 54.3 us; the launch traced here: 54.1 us
  Pallas kernels  49.5 us (91%)
  local copies, waits for them, and re-layouts  3.04 us (6%)
  other arithmetic  1.52 us (3%)
    pallas_call x1, Pallas kernels, on_device(): pl.pallas_call(whole_kernel, out_shape=jax.ShapeDtypeStruct((leaves, nrhs...  49.5 us
    unnamed x7, local copies, waits for them, and re-layouts  3.04 us

profile of v1, /device:TPU:0, one launch (start us, length us, event | category | flops | bytes accessed | tf_op | source)
XLA Modules:
  0.0 54.1 jit_solution(11245699981281378390)
XLA Ops:
  0.0 0.0 copy-start
  0.0 0.7 %and_select_fusion.1 = (s32[32]{0:T(128)S(1)}, s32[32]{0:T(128)S(1)}) fusion(s32[32]{0:T(128)} %param.11), kind=kLoop, calls=%fused_computation.7 | loop fusion | flops 608 | bytes 384 | tf_op jit(solution)/shard_map/jit(floor_divide)/jit(_where)/select_n | solution.py:390
  0.7 0.2 convert_reduce_fusion
  0.9 0.7 %select_reduce_fusion = (s32[32]{0:T(128)}, s32[32]{0:T(128)}) fusion(s32[32]{0:T(128)S(1)} %get-tuple-element.8, s32[32]{0:T(128)S(1)} %multiply_add_fusion), kind=kLoop, calls=%fused_computation | loop fusion | flops 5056 | bytes 512 | tf_op jit(solution)/shard_map/reduce_sum | solution.py:396
  1.5 0.0 copy-done
  1.5 0.0 copy-start.1
  1.5 0.7 %copy.13.near_list = s32[32,16]{1,0:T(8,128)} copy(s32[32,16]{0,1:T(8,128)S(1)} %copy-done) | data formatting | bytes 4096 | tf_op args[3]
  2.2 0.0 copy-done.1
  2.2 0.7 %copy.14.far_list = s32[32,16]{1,0:T(8,128)} copy(s32[32,16]{0,1:T(8,128)S(1)} %copy-done.1) | data formatting | bytes 4096 | tf_op args[4]
  2.9 49.5 %whole.1 = bf16[32,32,128]{2,1,0:T(8,128)(2,1)} custom-call(s32[32]{0:T(128)} %get-tuple-element.6.picks, s32[32]{0:T(128)} %get-tuple-element.5.slots, s32[32,16]{1,0:T(8,128)} %copy.13.near_list, s32[32,16]{1,0:T(8,128)} %copy.14.far_list, s32[4,32]{1,0:T(4,128)} %node_list.1, bf16[32,32,128]{2,1,0:T(8,128)(2,1)} %density.1, f32[6,4096]{1,0:T(8,128)} %geo.1, ...), custom_call_target="tpu_custom_call" | custom-call | tf_op jit(solution)/shard_map/whole/pallas_call | solution.py:402
  52.4 1.7 %copy.16 = bf16[32,32,128]{2,1,0:T(8,128)(2,1)} copy(bf16[32,32,128]{2,1,0:T(8,128)(2,1)} %whole.1) | data formatting | bytes 524288
  (1 shorter events, 0.0 us)
Async XLA Ops:
  0.0 1.5 %copy-start = (s32[32,16]{0,1:T(8,128)S(1)}, s32[32,16]{0,1:T(8,128)}, u32[]{:S(2)}) copy-start(s32[32,16]{0,1:T(8,128)} %param.13) | copy-start | bytes 6148
  1.5 0.7 %copy-start.1 = (s32[32,16]{0,1:T(8,128)S(1)}, s32[32,16]{0,1:T(8,128)}, u32[]{:S(2)}) copy-start(s32[32,16]{0,1:T(8,128)} %param.14) | copy-start | bytes 6148

commit v2 on v1

--- a/solution.py
+++ b/solution.py
@@ -13,7 +13,7 @@
 inv_four_pi = 0.25 / math.pi
 NT = (((1,), (1,)), ((), ()))
 bf16, f32 = jnp.bfloat16, jnp.float32
-EARLY, MIDDLE = 8, 16
+EARLY, MIDDLE = 0, 20
 
 
 def thirds(a):
@@ -53,6 +53,8 @@
 
 
 def each(lo, hi, group, body):
+    if hi <= lo:
+        return
     while (hi - lo) % group:
         group //= 2
 
@@ -65,10 +67,10 @@
 
 
 def whole_kernel(
-    picks, slots, near_list, far_list, node_list, density, geo, node_pts, basis_in_far, transfer_far,
+    near_list, far_list, node_list, leaf_target, density, geo, node_pts, basis_in_far, transfer_far,
     basis_out_far, out,
-    basis_in, transfer, basis_out, local_sem, outgoing, slot_rows, arrived, arrived_rows, geo_wide, dens_wide,
-    skel_wide, all_skel, near_src, near_tgt, far_src, far_tgt, far_skel, near_k, far_k, down, send_sem, recv_sem,
+    basis_in, transfer, local_sem, outgoing, slot_rows, arrived, arrived_rows, geo_wide, dens_wide,
+    skel_wide, all_skel, near_src, near_tgt, far_src, far_tgt, far_skel, near_k, far_k, down, local, send_sem, recv_sem,
 ):
     leaves, nrhs, size = out.shape
     here, rank, width = transfer.shape
@@ -107,24 +109,35 @@
     def columns(ref, block):
         return ref[:, pl.ds(pl.multiple_of(block * size, size), size)]
 
+    near_slots, far_slots, node_slots = near_list.shape[0], far_list.shape[0], node_list.shape[1]
+    near_rows = near_slots * size
     barrier = pltpu.get_barrier_semaphore()
     for k in range(1, count):
         pl.semaphore_signal(barrier, inc=1, device_id=peer(k)[1], device_id_type=pl.DeviceIdType.MESH)
     fetches = []
     for k, (src, dst) in enumerate(
-        ((basis_in_far, basis_in), (transfer_far, transfer), (basis_out_far, basis_out))
+        ((basis_in_far, basis_in), (transfer_far, transfer), (basis_out_far, near_k.at[:, pl.ds(near_rows, rank)]))
     ):
         fetch = pltpu.make_async_copy(src, dst, local_sem.at[k])
         fetch.start()
         fetches.append(fetch)
 
+    shift = leaves.bit_length() - 1
+    target = leaf_target[...]
+    leaf_row = lax.broadcasted_iota(jnp.int32, (leaves, leaves), 0)
+    leaf_col = lax.broadcasted_iota(jnp.int32, (leaves, leaves), 1)
+    target_down = jnp.sum(jnp.where(leaf_row == leaf_col, target, 0), axis=1, keepdims=True)
+    owner, owner_down = target >> shift, target_down >> shift
+    earlier = jnp.where((owner_down == owner) & (leaf_row > leaf_col), 1, 0)
+    rank_down = jnp.sum(earlier, axis=1, keepdims=True)
+    picks = jnp.sum(jnp.where(owner_down * per + rank_down == leaf_col, leaf_row, 0), axis=0, keepdims=True)
+    slot_hit = (target_down & (leaves - 1)) == lane
+    mark = jnp.where(slot_hit, me * per + rank_down + 1, 0)
+    for q in range(count):
+        slot_rows[q] = jnp.sum(jnp.where(owner_down == q, mark, 0), axis=0, keepdims=True)
     for j in range(leaves):
-        outgoing[j] = density[jnp.clip(picks[j], 0, leaves - 1)]
-    for q in range(count):
-        line = jnp.zeros((1, size), jnp.int32)
-        for k in range(per):
-            line = line + jnp.where(lane == slots[q * per + k], me * per + k + 1, 0)
-        slot_rows[q] = line
+        pick = jnp.max(jnp.where(leaf_col[:1] == j, picks, 0))
+        outgoing[j] = density[jnp.clip(pick, 0, leaves - 1)]
     geo_wide[0:6, halo : halo + inner] = geo[...]
 
     def turned(form):
@@ -145,6 +158,53 @@
 
     each(0, nodes // 2, 4, node_block)
 
+    def store_far_target(index, low_form, high_form):
+        gap = jnp.zeros((rank - low_form.shape[0], size), f32)
+        none = jnp.zeros((2 * rank, size), f32)
+        block = jnp.concatenate([low_form, gap, high_form, gap], axis=0)
+        far_tgt[index] = jnp.concatenate(
+            [jnp.concatenate([block, none], axis=0), jnp.concatenate([none, block], axis=0)], axis=1
+        ).astype(bf16)
+
+    def target_block(t):
+        form = left_side(target_form(columns(geo_wide, t + REACH), row))
+        terms = form.shape[0]
+        near_tgt[t] = jnp.concatenate(
+            [
+                jnp.concatenate([form, jnp.zeros((size - terms, size), f32)], axis=0),
+                jnp.concatenate(
+                    [jnp.zeros((terms, size), f32), form, jnp.zeros((size - 2 * terms, size), f32)], axis=0
+                ),
+            ],
+            axis=1,
+        ).astype(bf16)
+        store_far_target(t, jnp.where(low, form, 0.0), jnp.where(low, 0.0, pltpu.roll(form, rank, 1)))
+
+    def source_block(s):
+        points = columns(geo_wide, s)
+        xyz, source = source_form(points, row)
+        normal = jnp.where(row < 3, pltpu.roll(points, 5, 0), 0.0) * inv_four_pi
+        shift = -jnp.sum(normal * xyz, axis=0, keepdims=True)
+        normal = jnp.where(row == 4, shift, normal)
+        left = right_side(source)
+        form = turned(jnp.concatenate([left, right_side(normal)], axis=0))
+        near_src[s] = form.astype(bf16)
+        store_far_source(s, jnp.where(lane < left.shape[0], form[:rank], 0.0))
+
+    each(0, leaves, 4, target_block)
+    for b in range(here // 2):
+        form = left_side(
+            target_form(
+                jnp.concatenate(
+                    [columns(node_pts, me * (here // 2) + b), jnp.zeros((5, size), f32)], axis=0
+                ),
+                row,
+            )
+        )
+        other = pltpu.roll(form, rank, 1)
+        store_far_target(leaves + 2 * b, jnp.where(low, form, 0.0), jnp.where(low, 0.0, other))
+        store_far_target(leaves + 2 * b + 1, jnp.where(low, other, 0.0), jnp.where(low, 0.0, form))
+    each(REACH, REACH + leaves, 4, source_block)
     pl.semaphore_wait(barrier, count - 1)
     geo_copies = [
         send(geo.at[:, pl.ds(inner - halo, halo)], geo_wide.at[pl.ds(0, 6), pl.ds(0, halo)], peer(1)[1]),
@@ -161,66 +221,14 @@
     for k in range(per):
         arrived[me * per + k] = outgoing[me * per + k]
 
-    def store_far_target(index, low_form, high_form):
-        gap = jnp.zeros((rank - low_form.shape[0], size), f32)
-        none = jnp.zeros((2 * rank, size), f32)
-        block = jnp.concatenate([low_form, gap, high_form, gap], axis=0)
-        far_tgt[index] = jnp.concatenate(
-            [jnp.concatenate([block, none], axis=0), jnp.concatenate([none, block], axis=0)], axis=1
-        ).astype(bf16)
-
-    def target_block(t):
-        form = left_side(target_form(columns(geo_wide, t + REACH), row))
-        terms = form.shape[0]
-        near_tgt[t] = jnp.concatenate(
-            [
-                jnp.concatenate([form, jnp.zeros((size - terms, size), f32)], axis=0),
-                jnp.concatenate(
-                    [jnp.zeros((terms, size), f32), form, jnp.zeros((size - 2 * terms, size), f32)], axis=0
-                ),
-            ],
-            axis=1,
-        ).astype(bf16)
-        store_far_target(t, jnp.where(low, form, 0.0), jnp.where(low, 0.0, pltpu.roll(form, rank, 1)))
-
-    def source_block(s):
-        points = columns(geo_wide, s)
-        xyz, source = source_form(points, row)
-        normal = jnp.where(row < 3, pltpu.roll(points, 5, 0), 0.0) * inv_four_pi
-        shift = -jnp.sum(normal * xyz, axis=0, keepdims=True)
-        normal = jnp.where(row == 4, shift, normal)
-        left = right_side(source)
-        form = turned(jnp.concatenate([left, right_side(normal)], axis=0))
-        near_src[s] = form.astype(bf16)
-        store_far_source(s, jnp.where(lane < left.shape[0], form[:rank], 0.0))
-
-    each(0, leaves, 4, target_block)
-    for b in range(here // 2):
-        form = left_side(
-            target_form(
-                jnp.concatenate(
-                    [columns(node_pts, me * (here // 2) + b), jnp.zeros((5, size), f32)], axis=0
-                ),
-                row,
-            )
-        )
-        other = pltpu.roll(form, rank, 1)
-        store_far_target(leaves + 2 * b, jnp.where(low, form, 0.0), jnp.where(low, 0.0, other))
-        store_far_target(leaves + 2 * b + 1, jnp.where(low, other, 0.0), jnp.where(low, 0.0, form))
-    each(REACH, REACH + leaves, 4, source_block)
-    for copy in geo_copies:
-        copy.wait_recv()
-    each(0, REACH, 4, source_block)
-    each(REACH + leaves, wide, 4, source_block)
-
     def within(entry, shift, pad, least, end):
         return jnp.where(entry < 0, pad, jnp.clip(entry + shift, least, end - 1))
 
     def near_place(t, k, pad):
-        return within(near_list[t, k], REACH - first_leaf, pad, 0, wide)
+        return within(near_list[k, t], REACH - first_leaf, pad, 0, wide)
 
     def far_place(t, k, pad):
-        return within(far_list[t, k], REACH - first_leaf, pad, 0, wide)
+        return within(far_list[k, t], REACH - first_leaf, pad, 0, wide)
 
     def node_place(p, k, pad):
         return within(node_list[p, k], base, pad, base - 1, base + nodes)
@@ -234,7 +242,6 @@
             square = jnp.dot(points, weights, preferred_element_type=f32)
             store(g, (inv_four_pi * lax.rsqrt(square)).astype(bf16))
 
-    far_slots, node_slots = far_list.shape[1], node_list.shape[1]
     per_tile = 16
     tiles = node_slots // per_tile
 
@@ -253,9 +260,11 @@
         couple(far_tgt[leaves + p], [node_place(p, k, own) for k in range(node_slots)], store)
 
     each(0, here, 2, couple_node)
-    each(0, leaves, 4, couple_leaf)
-
-    near_slots = near_list.shape[1]
+    for copy in geo_copies:
+        copy.wait_recv()
+    each(0, REACH, 4, source_block)
+    each(REACH + leaves, wide, 4, source_block)
+    each(0, leaves, 8, couple_leaf)
 
     def near_leaf(t):
         weights = near_tgt[t]
@@ -364,14 +373,19 @@
         for c in range(children):
             down[p * children + c] = spreading[:, c * rank : (c + 1) * rank]
 
+    def finish_far(t):
+        far = gathered([far_place(t, k, wide) for k in range(far_slots)], far_k[t])
+        local[t] = (far + down[t]).astype(bf16)
+
+    each(0, leaves, 8, finish_far)
+
     def finish(t):
-        far = gathered([far_place(t, k, wide) for k in range(far_slots)], far_k[t])
-        charge = jnp.concatenate([dens_wide[near_place(t, k, wide)] for k in range(near_slots)], axis=1)
-        near = jnp.dot(charge, near_k[t], preferred_element_type=f32)
-        local = (far + down[t]).astype(bf16)
-        out[t] = (near + jnp.dot(local, basis_out[t], preferred_element_type=f32)).astype(bf16)
-
-    each(0, leaves, 4, finish)
+        charge = jnp.concatenate(
+            [dens_wide[near_place(t, k, wide)] for k in range(near_slots)] + [local[t]], axis=1
+        )
+        out[t] = jnp.dot(charge, near_k[t], preferred_element_type=f32).astype(bf16)
+
+    each(0, leaves, 8, finish)
     for copy in copies:
         copy.wait_send()
 
@@ -386,14 +400,6 @@
     rows_n, cols_n = lax.axis_size("row"), lax.axis_size("col")
     count = rows_n * cols_n
     nodes = here * count
-    per = leaves // count
-    destination = leaf_target // leaves
-    ids = jnp.arange(leaves, dtype=jnp.int32)
-    earlier = (destination[:, None] == destination) & (ids[:, None] > ids)
-    order = destination * per + jnp.sum(earlier.astype(jnp.int32), axis=1)
-    placed = order == ids[:, None]
-    picks = jnp.sum(jnp.where(placed, ids, 0), axis=1)
-    slots = jnp.sum(jnp.where(placed, leaf_target % leaves, 0), axis=1)
     tiles = node_list.shape[1] // 16
     n_copies = 2 * (count - 1) + 2 + 4 + (rows_n - 1) + (cols_n - 1) + (rows_n - 1) * (cols_n - 1)
     smem = pl.BlockSpec(memory_space=pltpu.SMEM)
@@ -402,12 +408,11 @@
     return pl.pallas_call(
         whole_kernel,
         out_shape=jax.ShapeDtypeStruct((leaves, nrhs, size), bf16),
-        in_specs=[smem] * 5 + [vmem] * 3 + [away] * 3,
+        in_specs=[smem] * 3 + [vmem] * 4 + [away] * 3,
         out_specs=vmem,
         scratch_shapes=[
             pltpu.VMEM(basis_in.shape, bf16),
             pltpu.VMEM(transfer.shape, bf16),
-            pltpu.VMEM(basis_out.shape, bf16),
             pltpu.SemaphoreType.DMA((3,)),
             pltpu.VMEM((leaves, nrhs, size), bf16),
             pltpu.VMEM((count, 1, size), jnp.int32),
@@ -422,9 +427,10 @@
             pltpu.VMEM((2, wide + 1 + nodes, rank, size), bf16),
             pltpu.VMEM((leaves + here, 4 * rank, 4 * rank), bf16),
             pltpu.VMEM((2, wide + 1 + nodes, nrhs, size), bf16),
-            pltpu.VMEM((leaves, near_list.shape[1] * size, size), bf16),
+            pltpu.VMEM((leaves, near_list.shape[1] * size + rank, size), bf16),
             pltpu.VMEM((leaves + here * tiles, 4 * rank, 4 * rank), bf16),
             pltpu.VMEM((leaves, nrhs, rank), f32),
+            pltpu.VMEM((leaves, nrhs, rank), bf16),
             pltpu.SemaphoreType.DMA((n_copies,)),
             pltpu.SemaphoreType.DMA((n_copies,)),
         ],
@@ -433,8 +439,8 @@
         ),
         name="whole",
     )(
-        picks, slots, near_list, far_list, node_list, density, geometry, node_points, basis_in, transfer,
-        basis_out,
+        near_list.T, far_list.T, node_list, leaf_target.reshape(1, leaves), density, geometry, node_points,
+        basis_in, transfer, basis_out,
     )
 
 

time: 54.3 us -> 41.6 us (0.77)
  Pallas kernels: 49.5 us -> 39.7 us
  other arithmetic: 1.52 us -> 0 us
  local copies, waits for them, and re-layouts: 3.04 us -> 1.67 us
    pallas_call x1, Pallas kernels: 49.5 us -> 39.7 us  [on_device(): pl.pallas_call(whole_kernel, out_shape=jax.ShapeDtypeStruct((leaves, nrhs...]
    unnamed x7 -> x1, local copies, waits for them, and re-layouts: 3.04 us -> 1.67 us
    reduce_sum x2 -> x0, other arithmetic: 0.84 us -> none  [the longest x1 0.66 us: on_device(): slots = jnp.sum(jnp.where(placed, leaf_target % leaves, 0), axis=1)]
    select_n x1 -> x0, other arithmetic: 0.68 us -> none  [on_device(): destination = leaf_target // leaves]
where the time goes in v2:
time: 41.6 us; the launch traced here: 41.4 us
  Pallas kernels  39.7 us (95%)
  local copies, waits for them, and re-layouts  1.67 us (4%)
    pallas_call x1, Pallas kernels, on_device(): pl.pallas_call(whole_kernel, out_shape=jax.ShapeDtypeStruct((leaves, nrhs...  39.7 us
    unnamed x1, local copies, waits for them, and re-layouts  1.67 us

profile of v2, /device:TPU:0, one launch (start us, length us, event | category | flops | bytes accessed | tf_op | source)
XLA Modules:
  0.0 41.4 jit_solution(9907229922630562061)
XLA Ops:
  0.0 39.7 %whole.1 = bf16[32,32,128]{2,1,0:T(8,128)(2,1)} custom-call(s32[16,32]{1,0:T(8,128)} %bitcast.3, s32[16,32]{1,0:T(8,128)} %bitcast.4, s32[4,32]{1,0:T(4,128)} %node_list.1, s32[1,32]{1,0:T(1,128)} %bitcast.5, bf16[32,32,128]{2,1,0:T(8,128)(2,1)} %density.1, f32[6,4096]{1,0:T(8,128)} %geo.1, f32[3,4096]{1,0:T(4,128)} %node_pts.1, ...), custom_call_target="tpu_custom_call" | custom-call | tf_op jit(solution)/shard_map/whole/pallas_call | solution.py:408
  39.7 1.7 %copy.12 = bf16[32,32,128]{2,1,0:T(8,128)(2,1)} copy(bf16[32,32,128]{2,1,0:T(8,128)(2,1)} %whole.1) | data formatting | bytes 524288
